TPU v7x, 32 devices: a whole 2x2x4 slice. The times are simulated.
32 devices in a mesh: cfd: 16 (over z, x, core), ac: 2 (over y).
Axes of the slice: x: 2, y: 2, z: 4, core: 2. Of those that a mesh axis runs over, the one named last changes fastest.
Arguments:
- surface_raw: bfloat16 [5, 4096, 1024], P(None, ('cfd', 'ac')), may hold values from -6 to 6
- area_normals: bfloat16 [3, 4096], P(None, ('cfd', 'ac')), may hold values from -6 to 6
- kernel_weights: bfloat16 [2, 3, 2048, 4096], P(None, None, None, ('cfd', 'ac')), may hold values from -0.078125 to 0.078125
- block_map: int32 [2, 16, 16], P('ac', 'cfd'), may hold values from 0 to 15, as said below
- band_observers: int32 [16, 128], replicated, may hold values from 0 to 2047, as said below
- band_lags: int32 [16], replicated, may hold values from 0 to 511
Outputs:
- acoustic: float32 [2048, 512], P('cfd', 'ac')
Inputs may be any that keep to these rules, and one draw needn't show every extreme that they name: block_map[j, s, :] is a permutation of 0 to 15 for every j and s. `band_observers`: every observer appears exactly once.
All inputs are finite; a program needn't handle non-finite values.
Results may differ from a plain program's by a relative error of at most 0.0042.
Values may be sent and summed in bfloat16 or wider, within the bound.
A program may use at most 64 MiB of HBM per device.

v0:
```python
import jax
import jax.numpy as jnp
from jax import lax
from jax.sharding import PartitionSpec as P


def thickness(surface, normals):
    along = surface[2].astype(jnp.float32) * normals[0].astype(jnp.float32)[:, None]
    along = along + surface[3].astype(jnp.float32) * normals[1].astype(jnp.float32)[:, None]
    along = along + surface[4].astype(jnp.float32) * normals[2].astype(jnp.float32)[:, None]
    return (surface[1].astype(jnp.float32) * along).astype(jnp.bfloat16)


def rates(series):
    step = series[:, 1:].astype(jnp.float32) - series[:, :-1].astype(jnp.float32)
    first = jnp.zeros((series.shape[0], 1), jnp.float32)
    return jnp.concatenate([first, step], axis=1).astype(jnp.bfloat16)


def reorder_blocks(array, block_order, blocks):
    lead = array.shape[0]
    rest = array.shape[2:]
    grouped = array.reshape((lead, blocks, -1))
    picked = jnp.take(grouped, block_order, axis=1)
    return picked.reshape((lead, array.shape[1]) + rest)


def local(surface_raw, area_normals, kernel_weights, block_map, band_observers, band_lags):
    blocks = lax.axis_size("cfd")
    block_order = block_map[0, 0]
    thick = thickness(surface_raw, area_normals)
    outgoing = reorder_blocks(jnp.stack([thick, surface_raw[0]]), block_order, blocks)
    arrived = lax.all_to_all(outgoing, "cfd", split_axis=1, concat_axis=1, tiled=True)
    thickness_in = arrived[0]
    pressure_in = arrived[1]
    sources = jnp.stack([rates(thickness_in), rates(pressure_in), pressure_in])
    out_len = sources.shape[2] // 2
    tap_count = kernel_weights.shape[0]
    band_count = band_observers.shape[0]
    band_width = band_observers.shape[1]
    observer_count = kernel_weights.shape[2]

    def one_band(carry, band_index):
        delay = band_lags[band_index]
        start = band_index * band_width
        chosen = lax.dynamic_slice_in_dim(kernel_weights, start, band_width, 2)
        windows = jnp.stack(
            [
                lax.dynamic_slice_in_dim(sources, out_len - delay - shift_step, out_len, 2)
                for shift_step in range(tap_count)
            ]
        )
        contribution = jnp.einsum(
            "kcof,kcft->ot", chosen, windows, preferred_element_type=jnp.float32
        )
        return (carry, contribution)

    _, banded = lax.scan(one_band, 0, jnp.arange(band_count, dtype=jnp.int32))
    banded = banded.reshape(observer_count, out_len)
    flat_ids = band_observers.reshape(-1)
    inverse = (
        jnp.zeros((observer_count,), jnp.int32)
        .at[flat_ids]
        .set(jnp.arange(observer_count, dtype=jnp.int32))
    )
    partial_value = jnp.take(banded, inverse, axis=0)
    reduced = lax.psum_scatter(partial_value, "cfd", scatter_dimension=0, tiled=True)
    result = lax.psum_scatter(reduced, "ac", scatter_dimension=1, tiled=True)
    return result


def solution(mesh):
    placed = (
        P(None, ("cfd", "ac"), None),
        P(None, ("cfd", "ac")),
        P(None, None, None, ("cfd", "ac")),
        P("ac", "cfd", None),
        P(),
        P(),
    )
    return jax.shard_map(
        local, mesh=mesh, in_specs=placed, out_specs=P("cfd", "ac"), check_vma=False
    )
```

profile of v0, /device:TPU:0, one launch (start us, length us, event | category | flops | bytes accessed | tf_op | source)
XLA Modules:
  0.0 283.2 jit_solution(15173410977402433018)
XLA Ops:
  6.5 0.7 fusion.9
  7.2 0.7 compare_and_fusion.1
  7.9 0.8 bitcast_convert_fusion.2
  8.6 1.0 slice.49
  9.6 1.5 multiply_convert_fusion
  11.6 1.2 pad_maximum_fusion.1
  12.8 1.6 gather_fusion
  15.3 1.3 copy.23
  16.6 7.4 %all-to-all-start = ((bf16[2,128,1024]{2,0,1:T(2,128)(2,1)}), bf16[2,128,1024]{2,0,1:T(2,128)(2,1)S(1)}, u32[]{:S(2)}, u32[]{:S(2)}) async-start(bf16[2,128,1024]{2,0,1:T(2,128)(2,1)} %copy.23), calls=%async_computation | async-start | bytes 1048576 | tf_op jit(solution)/shard_map/all_to_all | solution.py:33
  24.1 8.0 %scatter_custom_fusion = s32[2048]{0:T(1024)S(1)} fusion(s32[2048]{0:T(1024)S(1)} %bitcast.65, s32[2048]{0:T(1024)S(1)} %iota.6, s32[]{:T(128)} %constant.110.clone.1), kind=kCustom, calls=%fused_computation.28 | custom fusion | bytes 8196 | tf_op jit(solution)/shard_map/scatter | solution.py:64
  32.2 6.1 %all-to-all-done = bf16[2,128,1024]{2,0,1:T(2,128)(2,1)S(1)} async-done(((bf16[2,128,1024]{2,0,1:T(2,128)(2,1)}), bf16[2,128,1024]{2,0,1:T(2,128)(2,1)S(1)}, u32[]{:S(2)}, u32[]{:S(2)}) %all-to-all-start) | async-done | bytes 524320 | tf_op jit(solution)/shard_map/all_to_all | solution.py:33
  38.3 0.7 fusion.10
  40.0 135.3 %while.14 = (s32[]{:T(128)}, f32[16,128,512]{2,1,0:T(8,128)}, s32[16]{0:T(128)S(1)}, bf16[2,3,2048,128]{3,2,1,0:T(8,128)(2,1)}, s32[16]{0:T(128)S(1)}, /*index=5...) while((s32[]{:T(128)}, f32[16,128,512]{2,1,0:T(8,128)}, ...), condition=%wide.region_2.3_spmd, body=%wide.region_1.2_spmd.sunk | while | flops 101056528 | bytes 2818909 | solution.py:58
  40.0 0.6 dynamic_slice.57
  42.5 0.6 dynamic_slice.58
  46.5 1.9 fusion.16
  48.5 0.6 dynamic_slice.57
  50.9 0.6 dynamic_slice.58
  55.0 1.9 fusion.16
  56.9 0.6 dynamic_slice.57
  59.4 0.6 dynamic_slice.58
  63.5 1.9 fusion.16
  65.4 0.6 dynamic_slice.57
  67.8 0.6 dynamic_slice.58
  71.9 1.9 fusion.16
  73.8 0.6 dynamic_slice.57
  76.3 0.6 dynamic_slice.58
  80.4 1.9 fusion.16
  82.3 0.6 dynamic_slice.57
  84.7 0.6 dynamic_slice.58
  88.8 1.9 fusion.16
  90.7 0.6 dynamic_slice.57
  93.2 0.6 dynamic_slice.58
  97.3 1.9 fusion.16
  99.2 0.6 dynamic_slice.57
  101.6 0.6 dynamic_slice.58
  105.7 1.9 fusion.16
  107.6 0.6 dynamic_slice.57
  110.1 0.6 dynamic_slice.58
  114.2 1.9 fusion.16
  116.1 0.6 dynamic_slice.57
  118.5 0.6 dynamic_slice.58
  122.6 1.9 fusion.16
  124.6 0.6 dynamic_slice.57
  127.0 0.6 dynamic_slice.58
  131.1 1.9 fusion.16
  133.0 0.6 dynamic_slice.57
  135.5 0.6 dynamic_slice.58
  139.5 1.9 fusion.16
  141.5 0.6 dynamic_slice.57
  143.9 0.6 dynamic_slice.58
  148.0 1.9 fusion.16
  149.9 0.6 dynamic_slice.57
  152.4 0.6 dynamic_slice.58
  156.5 1.9 fusion.16
  158.4 0.6 dynamic_slice.57
  160.8 0.6 dynamic_slice.58
  164.9 1.9 fusion.16
  166.8 0.6 dynamic_slice.57
  173.4 1.9 fusion.16
  175.3 11.7 %gather_fusion.1 = f32[2048,512]{1,0:T(8,128)} fusion(f32[2048,512]{1,0:T(8,128)} %bitcast.60, s32[2048]{0:T(1024)S(1)} %fusion.6), kind=kCustom, calls=%fused_computation.1 | custom fusion | bytes 8396800 | tf_op jit(solution)/shard_map/jit(_take)/gather | solution.py:66
  187.0 3.8 %broadcast_select_fusion = f32[2048,512]{1,0:T(8,128)} fusion(f32[2048,512]{1,0:T(8,128)} %gather_fusion.1, pred[2048]{0:T(1024)(128)(4,1)S(1)} %compare_and_fusion), kind=kLoop, calls=%fused_computation.13 | loop fusion | flops 1048576 | bytes 8390656 | tf_op jit(solution)/shard_map/jit(_take)/select_n | solution.py:66
  190.9 72.4 %reduce-scatter.3.cloned.1.call-done = f32[128,512]{1,0:T(8,128)} async-done(((f32[2048,512]{1,0:T(8,128)}), f32[128,512]{1,0:T(8,128)}) %reduce-scatter.3.cloned.1.call-update) | async-done | bytes 262160 | tf_op jit(solution)/shard_map/reduce_scatter | solution.py:67
  263.3 13.0 %reduce-scatter.5.cloned.1.call-done = f32[128,256]{1,0:T(8,128)} async-done(((f32[128,512]{1,0:T(8,128)}), f32[128,256]{1,0:T(8,128)}) %reduce-scatter.5.cloned.1.call-update) | async-done | bytes 131088 | tf_op jit(solution)/shard_map/reduce_scatter | solution.py:68
  (46 shorter events, 9.2 us)
Async XLA Ops:
  11.3 12.7 %copy-start = (s32[16,128]{1,0:T(8,128)S(1)}, s32[16,128]{1,0:T(8,128)}, u32[]{:S(2)}) copy-start(s32[16,128]{1,0:T(8,128)} %param.12) | copy-start | bytes 24580
  16.6 21.7 %all-to-all-start = ((bf16[2,128,1024]{2,0,1:T(2,128)(2,1)}), bf16[2,128,1024]{2,0,1:T(2,128)(2,1)S(1)}, u32[]{:S(2)}, u32[]{:S(2)}) async-start(bf16[2,128,1024]{2,0,1:T(2,128)(2,1)} %copy.23), calls=%async_computation | async-start | bytes 1048576 | tf_op jit(solution)/shard_map/all_to_all | solution.py:33
  24.0 239.3 %reduce-scatter.3.cloned.1.call-start = ((), (), s32[]{:S(2)}) async-start(), calls=%async_computation.3 | async-start | bytes 4456448 | tf_op jit(solution)/shard_map/reduce_scatter | solution.py:67
  32.2 7.8 %copy-start.1 = (s32[16]{0:T(128)S(1)}, s32[16]{0:T(128)}, u32[]{:S(2)}) copy-start(s32[16]{0:T(128)} %param.13) | copy-start | bytes 196
  190.8 85.5 %reduce-scatter.5.cloned.1.call-start = ((), (), s32[]{:S(2)}) async-start(), calls=%async_computation.4 | async-start | bytes 393216 | tf_op jit(solution)/shard_map/reduce_scatter | solution.py:68
Sparse Core Ops, SparseCore 0:
  190.9 72.3 reduce-scatter.2
  265.5 10.7 reduce-scatter.4
where the time goes:
time: 285 us; the launch traced here: 283 us
  waiting for transfers between devices  91.6 us (32%)
  loops' own time  79.1 us (28%)
  local copies, waits for them, and re-layouts  51.7 us (18%)
  matrix products  30.7 us (11%)
  between operations  13.6 us (5%)
  other arithmetic  9.09 us (3%)
  starting transfers between devices  7.47 us (3%)
    another operation x1, loops' own time, local(): _, banded = lax.scan(one_band, 0, jnp.arange(band_count, dtype=jnp.int32))  79.1 us
    reduce_scatter x1, waiting for transfers between devices, local(): lax.psum_scatter(partial_value, 'cfd', scatter_dimension=0, tiled=True)  72.4 us
    dot_general x16, matrix products, one_band(): jnp.einsum('kcof,kcft->ot', chosen, windows, preferred_element_type=jnp.f...  30.7 us
    reduce_scatter x1, waiting for transfers between devices, local(): result = lax.psum_scatter(reduced, 'ac', scatter_dimension=1, tiled=True)  13 us
    gather x1, local copies, waits for them, and re-layouts, local(): partial_value = jnp.take(banded, inverse, axis=0)  11.7 us
    dynamic_slice x16, local copies, waits for them, and re-layouts, local(): _, banded = lax.scan(one_band, 0, jnp.arange(band_count, dtype=jnp.int32))  9.81 us
    dynamic_slice x16, local copies, waits for them, and re-layouts, one_band(): delay = band_lags[band_index]  9.56 us
    scatter x1, local copies, waits for them, and re-layouts, local(): inverse = jnp.zeros((observer_count,), jnp.int32).at[flat_ids].set(jnp.ar...  8.05 us
  transfers between devices with their start and end apart: 3, of which 3 were waited for; matrix products, arithmetic and copies ran while one was open for 3% of the time, Pallas kernels for 0%

commit v1 on v0

v1 whole, which is shorter than its diff:
```python
import functools

import jax
import jax.numpy as jnp
from jax import lax
from jax.experimental import pallas as pl
from jax.experimental.pallas import tpu as pltpu
from jax.sharding import PartitionSpec as P

LANES = 128


def prepare_kernel(src_ref, normals_ref, surface_ref, out_ref):
    along = surface_ref[2].astype(jnp.float32) * normals_ref[:, 0:1]
    along = along + surface_ref[3].astype(jnp.float32) * normals_ref[:, 1:2]
    along = along + surface_ref[4].astype(jnp.float32) * normals_ref[:, 2:3]
    thick = (surface_ref[1].astype(jnp.float32) * along).astype(jnp.bfloat16)
    both = jnp.concatenate([thick, surface_ref[0]], axis=0)
    rows = both.shape[0]
    column = lax.broadcasted_iota(jnp.int32, (rows, rows), 1)
    onehot = jnp.where(column == src_ref[...], 1.0, 0.0).astype(jnp.bfloat16)
    picked = jnp.dot(onehot, both, preferred_element_type=jnp.float32)
    out_ref[...] = picked.astype(jnp.bfloat16)


def prepare(surface_raw, area_normals, block_order):
    faces, steps = surface_raw.shape[1:]
    blocks = block_order.shape[0]
    size = faces // blocks
    src = (
        jnp.arange(2, dtype=jnp.int32)[None, :, None] * faces
        + block_order[:, None, None] * size
        + jnp.arange(size, dtype=jnp.int32)[None, None, :]
    ).reshape(2 * faces, 1)
    return pl.pallas_call(
        prepare_kernel,
        out_shape=jax.ShapeDtypeStruct((2 * faces, steps), jnp.bfloat16),
        name="prepare",
    )(src, area_normals.T.astype(jnp.float32), surface_raw)


def scatter_bands(lags_ref, ids_ref, arrived_ref, weights_ref, sources, band, rows):
    index = pl.program_id(0)
    taps, terms, width, faces = weights_ref.shape
    steps = sources.shape[1]
    out_len = steps // 2
    chunks = out_len // LANES

    @pl.when(index == 0)
    def _():
        series = arrived_ref[...].astype(jnp.float32)
        if len(arrived_ref.shape) == 4:
            thick = series[:, 0].reshape(faces, steps)
            pressure = series[:, 1].reshape(faces, steps)
        else:
            thick, pressure = series[:faces], series[faces:]
        step = lax.broadcasted_iota(jnp.int32, (faces, steps), 1)

        def rate(x):
            moved = jnp.where(step > 0, x - pltpu.roll(x, 1, 1), 0.0)
            return moved.astype(jnp.bfloat16).astype(jnp.float32)

        for c, x in enumerate((rate(thick), rate(pressure), pressure)):
            for k in range(taps):
                late = pltpu.roll(x, k, 1) if k else x
                sources[pl.ds((k * terms + c) * faces, faces), :] = late.astype(jnp.bfloat16)

    start = out_len - lags_ref[index]
    tile = jnp.minimum(start // LANES, steps // LANES - chunks - 1)
    rest = start - tile * LANES
    shift = lax.rem(LANES - rest, LANES)
    chosen = jnp.concatenate(
        [weights_ref[k, c] for k in range(taps) for c in range(terms)], axis=1
    )
    window = sources[:, pl.ds(pl.multiple_of(tile * LANES, LANES), out_len + LANES)]
    wide = jnp.dot(chosen, window, preferred_element_type=jnp.float32)
    lane = lax.broadcasted_iota(jnp.int32, (width, LANES), 1)
    parts = [
        pltpu.roll(wide[:, t * LANES : (t + 1) * LANES], shift, 1) for t in range(chunks + 1)
    ]
    for t in range(chunks):
        band[pl.ds(t, width, stride=chunks), :] = jnp.where(
            lane < LANES - rest, parts[t], parts[t + 1]
        )

    unroll = 16

    @pl.loop(0, width // unroll)
    def _(group):
        for m in range(unroll):
            slot = group * unroll + m
            place = ids_ref[index * width + slot]
            rows[pl.ds(pl.multiple_of(place * chunks, chunks), chunks), :] = band[
                pl.ds(pl.multiple_of(slot * chunks, chunks), chunks), :
            ]


def whole_kernel(lags_ref, ids_ref, arrived_ref, weights_ref, out_ref, sources, band, rows):
    scatter_bands(lags_ref, ids_ref, arrived_ref, weights_ref, sources, band, rows)
    observers, out_len = out_ref.shape
    chunks = out_len // LANES

    @pl.when(pl.program_id(0) == pl.num_programs(0) - 1)
    def _():
        for t in range(chunks):
            out_ref[:, t * LANES : (t + 1) * LANES] = rows[pl.ds(t, observers, stride=chunks), :]


def banded_call(kernel, outs, arrived, kernel_weights, band_observers, band_lags):
    taps, terms, observers, faces = kernel_weights.shape
    bands, width = band_observers.shape
    steps = arrived.shape[-1]
    chunks = steps // 2 // LANES
    rank = len(arrived.shape)
    return pl.pallas_call(
        kernel,
        out_shape=outs,
        grid_spec=pltpu.PrefetchScalarGridSpec(
            num_scalar_prefetch=2,
            grid=(bands,),
            in_specs=[
                pl.BlockSpec(arrived.shape, lambda b, *_: (0,) * rank),
                pl.BlockSpec((taps, terms, width, faces), lambda b, *_: (0, 0, b, 0)),
            ],
            out_specs=jax.tree.map(
                lambda o: pl.BlockSpec(o.shape, lambda b, *_: (0,) * len(o.shape)), outs
            ),
            scratch_shapes=[
                pltpu.VMEM((taps * terms * faces, steps), jnp.bfloat16),
                pltpu.VMEM((width * chunks, LANES), jnp.float32),
                pltpu.VMEM((observers * chunks, LANES), jnp.float32),
            ],
        ),
        compiler_params=pltpu.CompilerParams(dimension_semantics=("arbitrary",)),
        name="bands",
    )(band_lags, band_observers.reshape(-1), arrived, kernel_weights)


def local(surface_raw, area_normals, kernel_weights, block_map, band_observers, band_lags):
    blocks = lax.axis_size("cfd")
    faces, steps = surface_raw.shape[1:]
    size = faces // blocks
    outgoing = prepare(surface_raw, area_normals, block_map[0, 0])
    arrived = lax.all_to_all(outgoing, "cfd", split_axis=0, concat_axis=0, tiled=True)
    arrived = arrived.reshape(blocks, 2, size, steps)
    if size % 8:
        arrived = arrived.transpose(1, 0, 2, 3).reshape(2 * faces, steps)
    partial_value = banded_call(
        whole_kernel,
        jax.ShapeDtypeStruct((kernel_weights.shape[2], steps // 2), jnp.float32),
        arrived,
        kernel_weights,
        band_observers,
        band_lags,
    )
    reduced = lax.psum_scatter(partial_value, "cfd", scatter_dimension=0, tiled=True)
    return lax.psum_scatter(reduced, "ac", scatter_dimension=1, tiled=True)


def solution(mesh):
    placed = (
        P(None, ("cfd", "ac"), None),
        P(None, ("cfd", "ac")),
        P(None, None, None, ("cfd", "ac")),
        P("ac", "cfd", None),
        P(),
        P(),
    )
    return jax.shard_map(
        local, mesh=mesh, in_specs=placed, out_specs=P("cfd", "ac"), check_vma=False
    )
```

time: 285 us -> 144 us (0.51)
  loops' own time: 79.1 us -> 0 us
  local copies, waits for them, and re-layouts: 51.7 us -> 2.19 us
  matrix products: 30.7 us -> 0 us
  blocking collectives: 0 us -> 21.8 us
  Pallas kernels: 0 us -> 19.9 us
  other arithmetic: 9.09 us -> 0.81 us
  starting transfers between devices: 7.47 us -> 0.04 us
  waiting for transfers between devices: 91.6 us -> 85.5 us
    another operation x1 -> x0, loops' own time: 79.1 us -> none  [local(): _, banded = lax.scan(one_band, 0, jnp.arange(band_count, dtype=jnp.int32))]
    dot_general x16 -> x0, matrix products: 30.7 us -> none  [one_band(): jnp.einsum('kcof,kcft->ot', chosen, windows, preferred_element_type=jnp.f...]
    all_to_all x0 -> x1, blocking collectives: none -> 21.8 us  [local(): lax.all_to_all(outgoing, 'cfd', split_axis=0, concat_axis=0, tiled=True)]
    pallas_call x0 -> x2, Pallas kernels: none -> 19.9 us  [the longest x1 17.2 us: banded_call(): pl.pallas_call(kernel, out_shape=outs, grid_spec=pltpu.PrefetchScalarGrid...]
    dynamic_slice x32 -> x0, local copies, waits for them, and re-layouts: 19.4 us -> none  [the longest x16 9.81 us: local(): _, banded = lax.scan(one_band, 0, jnp.arange(band_count, dtype=jnp.int32))]
    gather x4 -> x0, local copies, waits for them, and re-layouts: 13.9 us -> none  [the longest x1 11.7 us: local(): partial_value = jnp.take(banded, inverse, axis=0)]
    scatter x1 -> x0, local copies, waits for them, and re-layouts: 8.05 us -> none  [local(): inverse = jnp.zeros((observer_count,), jnp.int32).at[flat_ids].set(jnp.ar...]
    all_to_all x1 -> x0, starting transfers between devices: 7.39 us -> none  [local(): lax.all_to_all(outgoing, 'cfd', split_axis=1, concat_axis=1, tiled=True)]
  transfers between devices with their start and end apart: 3 -> 2, of which waited for: 3 -> 2; matrix products, arithmetic and copies ran while one was open for 3% -> 0% of each run, Pallas kernels for 0% -> 0%
where the time goes in v1:
time: 144 us
  waiting for transfers between devices  85.5 us (59%)
  blocking collectives  21.8 us (15%)
  Pallas kernels  19.9 us (14%)
  between operations  13.4 us (9%)
  local copies, waits for them, and re-layouts  2.19 us (2%)
    reduce_scatter x1, waiting for transfers between devices, local(): lax.psum_scatter(partial_value, 'cfd', scatter_dimension=0, tiled=True)  72.4 us
    all_to_all x1, blocking collectives, local(): lax.all_to_all(outgoing, 'cfd', split_axis=0, concat_axis=0, tiled=True)  21.8 us
    pallas_call x1, Pallas kernels, banded_call(): pl.pallas_call(kernel, out_shape=outs, grid_spec=pltpu.PrefetchScalarGrid...  17.2 us
    reduce_scatter x1, waiting for transfers between devices, local(): return lax.psum_scatter(reduced, 'ac', scatter_dimension=1, tiled=True)  13.1 us
  transfers between devices with their start and end apart: 2, of which 2 were waited for; matrix products, arithmetic and copies ran while one was open for 0% of the time, Pallas kernels for 0%

profile of v1, /device:TPU:0, one launch (start us, length us, event | category | flops | bytes accessed | tf_op | source)
XLA Modules:
  0.0 143.7 jit_solution(17171392308742701531)
XLA Ops:
  6.5 0.0 reduce-scatter.3.cloned.1.call-start
  6.5 0.7 multiply_bitcast_fusion
  7.2 0.1 broadcast_add_fusion
  7.3 0.1 iota_add_fusion
  7.4 1.4 copy.8
  8.8 0.8 add.52.src_ref
  9.6 2.7 %prepare.1 = bf16[256,1024]{1,0:T(8,128)(2,1)} custom-call(s32[256,1]{1,0:T(8,128)} %add.52.src_ref, f32[128,3]{1,0:T(8,128)} %bitcast.8, bf16[5,128,1024]{2,1,0:T(8,128)(2,1)} %surface_ref.1), custom_call_target="tpu_custom_call" | custom-call | tf_op jit(solution)/shard_map/prepare/pallas_call | solution.py:35
  12.3 21.8 %all_to_all.9 = bf16[16,16,1024]{2,1,0:T(8,128)(2,1)} all-to-all(bf16[16,16,1024]{2,1,0:T(8,128)(2,1)} %bitcast.7), channel_id=1, replica_groups=mesh['cfd'=16,'ac'=2] {'cfd'}, dimensions={0} | all-to-all | bytes 1048576 | tf_op jit(solution)/shard_map/all_to_all | solution.py:144
  34.0 17.2 %bands.1 = f32[2048,512]{1,0:T(8,128)} custom-call(s32[16]{0:T(128)} %lags_ref.1, s32[2048]{0:T(1024)} %bitcast.9, bf16[16,2,8,1024]{3,2,1,0:T(8,128)(2,1)} %bitcast.6, bf16[2,3,2048,128]{3,2,1,0:T(8,128)(2,1)} %weights_ref.1), custom_call_target="tpu_custom_call" | custom-call | tf_op jit(solution)/shard_map/bands/pallas_call | solution.py:115
  51.3 0.0 reduce-scatter.3.cloned.1.call-update
  51.3 0.0 reduce-scatter.5.cloned.1.call-start
  51.3 72.4 %reduce-scatter.3.cloned.1.call-done = f32[128,512]{1,0:T(8,128)} async-done(((f32[2048,512]{1,0:T(8,128)}), f32[128,512]{1,0:T(8,128)}) %reduce-scatter.3.cloned.1.call-update) | async-done | bytes 262160 | tf_op jit(solution)/shard_map/reduce_scatter | solution.py:156
  123.7 0.0 reduce-scatter.5.cloned.1.call-update
  123.8 13.1 %reduce-scatter.5.cloned.1.call-done = f32[128,256]{1,0:T(8,128)} async-done(((f32[128,512]{1,0:T(8,128)}), f32[128,256]{1,0:T(8,128)}) %reduce-scatter.5.cloned.1.call-update) | async-done | bytes 131088 | tf_op jit(solution)/shard_map/reduce_scatter | solution.py:157
  (1 shorter events, 0.0 us)
Async XLA Ops:
  6.5 117.2 %reduce-scatter.3.cloned.1.call-start = ((), (), s32[]{:S(2)}) async-start(), calls=%async_computation.3 | async-start | bytes 4456448 | tf_op jit(solution)/shard_map/reduce_scatter | solution.py:156
  51.3 85.5 %reduce-scatter.5.cloned.1.call-start = ((), (), s32[]{:S(2)}) async-start(), calls=%async_computation.4 | async-start | bytes 393216 | tf_op jit(solution)/shard_map/reduce_scatter | solution.py:157
Sparse Core Ops, SparseCore 0:
  51.4 72.2 reduce-scatter.2
  126.0 10.8 reduce-scatter.4

commit v2 on v1

--- a/solution.py
+++ b/solution.py
@@ -136,6 +136,34 @@
     )(band_lags, band_observers.reshape(-1), arrived, kernel_weights)
 
 
+def halve(total, axis, bit):
+    size = lax.axis_size(axis)
+    mine = (lax.axis_index(axis) >> bit) & 1
+    if axis == "cfd":
+        owners, rows, times = total.shape
+        pairs = total.reshape(owners // 2, 2, rows, times)
+        first, second = pairs[:, 0], pairs[:, 1]
+    else:
+        first, second = jnp.split(total, 2, axis=2)
+    kept = jnp.where(mine == 1, second, first)
+    sent = jnp.where(mine == 1, first, second).astype(jnp.bfloat16)
+    partners = [(i, i ^ (1 << bit)) for i in range(size)]
+    return kept + lax.ppermute(sent, axis, partners).astype(jnp.float32)
+
+
+def exchange_sums(partial_value):
+    owners = lax.axis_size("cfd")
+    observers, times = partial_value.shape
+    near = [("cfd", b) for b in range(owners.bit_length() - 1)]
+    across = [("ac", b) for b in reversed(range(lax.axis_size("ac").bit_length() - 1))]
+    orders = (near[:2] + across + near[2:], near[:1] + across + near[1:])
+    total = halve(partial_value.reshape(owners, observers // owners, times), *near[0])
+    streams = jnp.split(total, len(orders), axis=1)
+    for step in range(1, len(near) + len(across)):
+        streams = [halve(part, *order[step]) for part, order in zip(streams, orders)]
+    return jnp.concatenate([part[0] for part in streams], axis=0)
+
+
 def local(surface_raw, area_normals, kernel_weights, block_map, band_observers, band_lags):
     blocks = lax.axis_size("cfd")
     faces, steps = surface_raw.shape[1:]
@@ -153,8 +181,7 @@
         band_observers,
         band_lags,
     )
-    reduced = lax.psum_scatter(partial_value, "cfd", scatter_dimension=0, tiled=True)
-    return lax.psum_scatter(reduced, "ac", scatter_dimension=1, tiled=True)
+    return exchange_sums(partial_value)
 
 
 def solution(mesh):

time: 144 us -> 81.2 us (0.56)
  waiting for transfers between devices: 85.5 us -> 28.6 us
  blocking collectives: 21.8 us -> 0 us
  starting transfers between devices: 0.04 us -> 20.8 us
  between operations: 13.4 us -> 0.14 us
  other arithmetic: 0.81 us -> 8.07 us
    reduce_scatter x2 -> x0, waiting for transfers between devices: 85.5 us -> none  [the longest x1 72.4 us: local(): lax.psum_scatter(partial_value, 'cfd', scatter_dimension=0, tiled=True)]
    all_to_all x1 -> x0, blocking collectives: 21.8 us -> none  [local(): lax.all_to_all(outgoing, 'cfd', split_axis=0, concat_axis=0, tiled=True)]
    ppermute x0 -> x9, waiting for transfers between devices: none -> 14.4 us  [halve(): return kept + lax.ppermute(sent, axis, partners).astype(jnp.float32)]
    all_to_all x0 -> x1, waiting for transfers between devices: none -> 14.3 us  [local(): lax.all_to_all(outgoing, 'cfd', split_axis=0, concat_axis=0, tiled=True)]
    ppermute x0 -> x9, starting transfers between devices: none -> 13.4 us  [halve(): return kept + lax.ppermute(sent, axis, partners).astype(jnp.float32)]
    all_to_all x0 -> x1, starting transfers between devices: none -> 7.39 us  [local(): lax.all_to_all(outgoing, 'cfd', split_axis=0, concat_axis=0, tiled=True)]
    convert_element_type x0 -> x9, other arithmetic: none -> 3.32 us  [halve(): sent = jnp.where(mine == 1, first, second).astype(jnp.bfloat16)]
    add x0 -> x5, other arithmetic: none -> 3.2 us  [halve(): return kept + lax.ppermute(sent, axis, partners).astype(jnp.float32)]
  transfers between devices with their start and end apart: 2 -> 10, of which waited for: 2 -> 7; matrix products, arithmetic and copies ran while one was open for 0% -> 1% of each run, Pallas kernels for 0% -> 0%
where the time goes in v2:
time: 81.2 us; the launch traced here: 80.6 us
  waiting for transfers between devices  28.6 us (35%)
  starting transfers between devices  20.8 us (26%)
  Pallas kernels  20 us (25%)
  other arithmetic  8.07 us (10%)
  local copies, waits for them, and re-layouts  3.04 us (4%)
    pallas_call x1, Pallas kernels, banded_call(): pl.pallas_call(kernel, out_shape=outs, grid_spec=pltpu.PrefetchScalarGrid...  17.3 us
    ppermute x9, waiting for transfers between devices, halve(): return kept + lax.ppermute(sent, axis, partners).astype(jnp.float32)  14.4 us
    all_to_all x1, waiting for transfers between devices, local(): lax.all_to_all(outgoing, 'cfd', split_axis=0, concat_axis=0, tiled=True)  14.3 us
    ppermute x9, starting transfers between devices, halve(): return kept + lax.ppermute(sent, axis, partners).astype(jnp.float32)  13.4 us
    all_to_all x1, starting transfers between devices, local(): lax.all_to_all(outgoing, 'cfd', split_axis=0, concat_axis=0, tiled=True)  7.39 us
    convert_element_type x9, other arithmetic, halve(): sent = jnp.where(mine == 1, first, second).astype(jnp.bfloat16)  3.32 us
    add x5, other arithmetic, halve(): return kept + lax.ppermute(sent, axis, partners).astype(jnp.float32)  3.2 us
    pallas_call x1, Pallas kernels, prepare(): pl.pallas_call(prepare_kernel, out_shape=jax.ShapeDtypeStruct((2 * faces,...  2.72 us
  transfers between devices with their start and end apart: 10, of which 7 were waited for; matrix products, arithmetic and copies ran while one was open for 1% of the time, Pallas kernels for 0%

profile of v2, /device:TPU:0, one launch (start us, length us, event | category | flops | bytes accessed | tf_op | source)
XLA Modules:
  0.0 80.6 jit_solution(17134980392425291757)
XLA Ops:
  0.0 0.7 multiply_bitcast_fusion
  0.7 0.1 broadcast_add_fusion
  0.7 0.1 iota_add_fusion
  0.8 0.8 add.84.src_ref
  1.6 1.4 %copy.32 = f32[3,128]{0,1:T(8,128)} copy(bf16[3,128]{1,0:T(4,128)(2,1)} %param.7) | data formatting | bytes 2304 | tf_op jit(solution)/shard_map/convert_element_type | solution.py:39
  3.0 2.7 %prepare.1 = bf16[256,1024]{1,0:T(8,128)(2,1)} custom-call(s32[256,1]{1,0:T(8,128)} %add.84.src_ref, f32[128,3]{1,0:T(8,128)} %bitcast.149, bf16[5,128,1024]{2,1,0:T(8,128)(2,1)} %surface_ref.1), custom_call_target="tpu_custom_call" | custom-call | tf_op jit(solution)/shard_map/prepare/pallas_call | solution.py:35
  5.7 7.4 %all-to-all-start = ((bf16[16,16,1024]{2,1,0:T(8,128)(2,1)}), bf16[16,16,1024]{2,1,0:T(8,128)(2,1)S(1)}, u32[]{:S(2)}, u32[]{:S(2)}) async-start(bf16[16,16,1024]{2,1,0:T(8,128)(2,1)} %bitcast.144), calls=%async_computation | async-start | bytes 1048576 | tf_op jit(solution)/shard_map/all_to_all | solution.py:172
  13.1 14.3 %all-to-all-done = bf16[16,16,1024]{2,1,0:T(8,128)(2,1)S(1)} async-done(((bf16[16,16,1024]{2,1,0:T(8,128)(2,1)}), bf16[16,16,1024]{2,1,0:T(8,128)(2,1)S(1)}, u32[]{:S(2)}, u32[]{:S(2)}) %all-to-all-start) | async-done | bytes 524320 | tf_op jit(solution)/shard_map/all_to_all | solution.py:172
  27.4 0.0 copy-start
  27.4 0.8 copy-done
  28.2 17.3 %bands.1 = f32[2048,512]{1,0:T(8,128)} custom-call(s32[16]{0:T(128)} %lags_ref.1, s32[2048]{0:T(1024)} %bitcast.150, bf16[16,2,8,1024]{3,2,1,0:T(8,128)(2,1)} %bitcast.143, bf16[2,3,2048,128]{3,2,1,0:T(8,128)(2,1)} %weights_ref.1), custom_call_target="tpu_custom_call" | custom-call | tf_op jit(solution)/shard_map/bands/pallas_call | solution.py:115
  45.4 2.4 %fusion = bf16[8,128,512]{2,1,0:T(8,128)(2,1)S(1)} fusion(f32[8,2,128,512]{3,2,1,0:T(8,128)} %bitcast.137, pred[]{:T(512)S(6)} %eq.14), kind=kLoop, calls=%fused_computation.4 | loop fusion | flops 524288 | bytes 3145729 | tf_op jit(solution)/shard_map/convert_element_type | solution.py:149
  47.9 0.2 collective-permute-start
  48.1 2.5 %collective-permute-done = bf16[8,128,512]{2,1,0:T(8,128)(2,1)S(1)} collective-permute-done((bf16[8,128,512]{2,1,0:T(8,128)(2,1)S(1)}, bf16[8,128,512]{2,1,0:T(8,128)(2,1)S(1)}, u32[]{:S(2)}, u32[]{:S(2)}) %collective-permute-start) | collective-permute-done | bytes 1048608 | tf_op jit(solution)/shard_map/ppermute | solution.py:151
  50.6 2.9 %bitcast_add_fusion = f32[8,128,512]{2,1,0:T(8,128)S(1)} fusion(bf16[8,128,512]{2,1,0:T(8,128)(2,1)S(1)} %collective-permute-done, f32[8,2,128,512]{3,2,1,0:T(8,128)} %bitcast.138, pred[]{:T(512)S(6)} %eq.14), kind=kLoop, calls=%fused_computation.2 | loop fusion | flops 1572864 | bytes 7340033 | tf_op jit(solution)/shard_map/add | solution.py:151
  53.5 0.1 split.21
  53.6 0.8 fusion.3
  54.3 1.0 %collective-permute-start.1 = (bf16[4,64,512]{2,1,0:T(8,128)(2,1)}, bf16[4,64,512]{2,1,0:T(8,128)(2,1)S(1)}, u32[]{:S(2)}, u32[]{:S(2)}) collective-permute-start(bf16[4,64,512]{2,1,0:T(8,128)(2,1)} %fusion.3), channel_id=1, source_target_pairs={{0,4},{2,6},{4,0},{6,2},{8,12},{10,14},{12,8},{14,10},{16,20},{18,... | collective-permute-start | bytes 786440 | tf_op jit(solution)/shard_map/ppermute | solution.py:151
  55.4 1.6 %collective-permute-start.5 = (bf16[8,64,256]{2,1,0:T(8,128)(2,1)S(1)}, bf16[8,64,256]{2,1,0:T(8,128)(2,1)S(1)}, u32[]{:S(2)}, u32[]{:S(2)}) collective-permute-start(bf16[8,64,256]{2,1,0:T(8,128)(2,1)S(1)} %select_convert_fusion.1), channel_id=1, source_target_pairs={{0,1},{1,0},{2,3},{3,2},{4,5},{5,4},{6,7},{7,6},{8,9},{9,8},{10,11... | collective-permute-start | bytes 786440 | tf_op jit(solution)/shard_map/ppermute | solution.py:151
  57.0 5.9 %collective-permute-done.1 = bf16[4,64,512]{2,1,0:T(8,128)(2,1)S(1)} collective-permute-done((bf16[4,64,512]{2,1,0:T(8,128)(2,1)}, bf16[4,64,512]{2,1,0:T(8,128)(2,1)S(1)}, u32[]{:S(2)}, u32[]{:S(2)}) %collective-permute-start.1) | collective-permute-done | bytes 262176 | tf_op jit(solution)/shard_map/ppermute | solution.py:151
  62.9 0.1 fusion.2
  63.1 1.6 %collective-permute-start.2 = (bf16[4,64,256]{2,1,0:T(8,128)(2,1)S(1)}, bf16[4,64,256]{2,1,0:T(8,128)(2,1)S(1)}, u32[]{:S(2)}, u32[]{:S(2)}) collective-permute-start(bf16[4,64,256]{2,1,0:T(8,128)(2,1)S(1)} %select_convert_fusion.4), channel_id=1, source_target_pairs={{0,1},{1,0},{2,3},{3,2},{4,5},{5,4},{6,7},{7,6},{8,9},{9,8},{10,11... | collective-permute-start | bytes 393224 | tf_op jit(solution)/shard_map/ppermute | solution.py:151
  64.6 0.0 collective-permute-done.5
  64.6 0.1 convert_add_fusion
  64.8 1.3 %collective-permute-start.6 = (bf16[4,64,256]{2,1,0:T(8,128)(2,1)S(1)}, bf16[4,64,256]{2,1,0:T(8,128)(2,1)S(1)}, u32[]{:S(2)}, u32[]{:S(2)}) collective-permute-start(bf16[4,64,256]{2,1,0:T(8,128)(2,1)S(1)} %fusion.6), channel_id=1, source_target_pairs={{0,4},{2,6},{4,0},{6,2},{8,12},{10,14},{12,8},{14,10},{16,20},{18,... | collective-permute-start | bytes 393224 | tf_op jit(solution)/shard_map/ppermute | solution.py:151
  66.1 2.0 %collective-permute-done.2 = bf16[4,64,256]{2,1,0:T(8,128)(2,1)S(1)} collective-permute-done((bf16[4,64,256]{2,1,0:T(8,128)(2,1)S(1)}, bf16[4,64,256]{2,1,0:T(8,128)(2,1)S(1)}, u32[]{:S(2)}, u32[]{:S(2)}) %collective-permute-start.2) | collective-permute-done | bytes 131104 | tf_op jit(solution)/shard_map/ppermute | solution.py:151
  68.2 1.8 %collective-permute-start.3 = (bf16[2,64,256]{2,1,0:T(8,128)(2,1)S(1)}, bf16[2,64,256]{2,1,0:T(8,128)(2,1)S(1)}, u32[]{:S(2)}, u32[]{:S(2)}) collective-permute-start(bf16[2,64,256]{2,1,0:T(8,128)(2,1)S(1)} %fusion.11), channel_id=1, source_target_pairs={{0,8},{2,10},{4,12},{6,14},{8,0},{10,2},{12,4},{14,6},{16,24},{18,... | collective-permute-start | bytes 196616 | tf_op jit(solution)/shard_map/ppermute | solution.py:151
  70.0 0.0 collective-permute-done.6
  70.1 1.6 %collective-permute-start.7 = (bf16[2,64,256]{2,1,0:T(8,128)(2,1)S(1)}, bf16[2,64,256]{2,1,0:T(8,128)(2,1)S(1)}, u32[]{:S(2)}, u32[]{:S(2)}) collective-permute-start(bf16[2,64,256]{2,1,0:T(8,128)(2,1)S(1)} %fusion.12), channel_id=1, source_target_pairs={{0,8},{2,10},{4,12},{6,14},{8,0},{10,2},{12,4},{14,6},{16,24},{18,... | collective-permute-start | bytes 196616 | tf_op jit(solution)/shard_map/ppermute | solution.py:151
  71.7 0.8 collective-permute-done.3
  72.5 2.5 %collective-permute-start.4 = (bf16[1,64,256]{2,1,0:T(8,128)(2,1)S(1)}, bf16[1,64,256]{2,1,0:T(8,128)(2,1)S(1)}, u32[]{:S(2)}, u32[]{:S(2)}) collective-permute-start(bf16[1,64,256]{2,1,0:T(8,128)(2,1)S(1)} %fusion.15), channel_id=1, source_target_pairs={{0,16},{2,18},{4,20},{6,22},{8,24},{10,26},{12,28},{14,30},{16,0},... | collective-permute-start | bytes 98312 | tf_op jit(solution)/shard_map/ppermute | solution.py:151
  75.0 0.0 collective-permute-done.7
  75.1 1.7 %collective-permute-start.8 = (bf16[1,64,256]{2,1,0:T(8,128)(2,1)S(1)}, bf16[1,64,256]{2,1,0:T(8,128)(2,1)S(1)}, u32[]{:S(2)}, u32[]{:S(2)}) collective-permute-start(bf16[1,64,256]{2,1,0:T(8,128)(2,1)S(1)} %fusion.16), channel_id=1, source_target_pairs={{0,16},{2,18},{4,20},{6,22},{8,24},{10,26},{12,28},{14,30},{16,0},... | collective-permute-start | bytes 98312 | tf_op jit(solution)/shard_map/ppermute | solution.py:151
  76.7 0.7 collective-permute-done.4
  77.4 2.5 %collective-permute-done.8 = bf16[1,64,256]{2,1,0:T(8,128)(2,1)S(1)} collective-permute-done((bf16[1,64,256]{2,1,0:T(8,128)(2,1)S(1)}, bf16[1,64,256]{2,1,0:T(8,128)(2,1)S(1)}, u32[]{:S(2)}, u32[]{:S(2)}) %collective-permute-start.8) | collective-permute-done | bytes 32800 | tf_op jit(solution)/shard_map/ppermute | solution.py:151
  79.9 0.7 pad_maximum_fusion
  (14 shorter events, 0.3 us)
Async XLA Ops:
  5.7 21.7 %all-to-all-start = ((bf16[16,16,1024]{2,1,0:T(8,128)(2,1)}), bf16[16,16,1024]{2,1,0:T(8,128)(2,1)S(1)}, u32[]{:S(2)}, u32[]{:S(2)}) async-start(bf16[16,16,1024]{2,1,0:T(8,128)(2,1)} %bitcast.144), calls=%async_computation | async-start | bytes 1048576 | tf_op jit(solution)/shard_map/all_to_all | solution.py:172
  27.4 0.8 copy-start
  47.9 2.7 %collective-permute-start = (bf16[8,128,512]{2,1,0:T(8,128)(2,1)S(1)}, bf16[8,128,512]{2,1,0:T(8,128)(2,1)S(1)}, u32[]{:S(2)}, u32[]{:S(2)}) collective-permute-start(bf16[8,128,512]{2,1,0:T(8,128)(2,1)S(1)} %fusion), channel_id=1, source_target_pairs={{0,2},{2,0},{4,6},{6,4},{8,10},{10,8},{12,14},{14,12},{16,18},{18,... | collective-permute-start | bytes 3145736 | tf_op jit(solution)/shard_map/ppermute | solution.py:151
  54.3 8.6 %collective-permute-start.1 = (bf16[4,64,512]{2,1,0:T(8,128)(2,1)}, bf16[4,64,512]{2,1,0:T(8,128)(2,1)S(1)}, u32[]{:S(2)}, u32[]{:S(2)}) collective-permute-start(bf16[4,64,512]{2,1,0:T(8,128)(2,1)} %fusion.3), channel_id=1, source_target_pairs={{0,4},{2,6},{4,0},{6,2},{8,12},{10,14},{12,8},{14,10},{16,20},{18,... | collective-permute-start | bytes 786440 | tf_op jit(solution)/shard_map/ppermute | solution.py:151
  55.4 9.2 %collective-permute-start.5 = (bf16[8,64,256]{2,1,0:T(8,128)(2,1)S(1)}, bf16[8,64,256]{2,1,0:T(8,128)(2,1)S(1)}, u32[]{:S(2)}, u32[]{:S(2)}) collective-permute-start(bf16[8,64,256]{2,1,0:T(8,128)(2,1)S(1)} %select_convert_fusion.1), channel_id=1, source_target_pairs={{0,1},{1,0},{2,3},{3,2},{4,5},{5,4},{6,7},{7,6},{8,9},{9,8},{10,11... | collective-permute-start | bytes 786440 | tf_op jit(solution)/shard_map/ppermute | solution.py:151
  63.1 5.0 %collective-permute-start.2 = (bf16[4,64,256]{2,1,0:T(8,128)(2,1)S(1)}, bf16[4,64,256]{2,1,0:T(8,128)(2,1)S(1)}, u32[]{:S(2)}, u32[]{:S(2)}) collective-permute-start(bf16[4,64,256]{2,1,0:T(8,128)(2,1)S(1)} %select_convert_fusion.4), channel_id=1, source_target_pairs={{0,1},{1,0},{2,3},{3,2},{4,5},{5,4},{6,7},{7,6},{8,9},{9,8},{10,11... | collective-permute-start | bytes 393224 | tf_op jit(solution)/shard_map/ppermute | solution.py:151
  64.8 5.2 %collective-permute-start.6 = (bf16[4,64,256]{2,1,0:T(8,128)(2,1)S(1)}, bf16[4,64,256]{2,1,0:T(8,128)(2,1)S(1)}, u32[]{:S(2)}, u32[]{:S(2)}) collective-permute-start(bf16[4,64,256]{2,1,0:T(8,128)(2,1)S(1)} %fusion.6), channel_id=1, source_target_pairs={{0,4},{2,6},{4,0},{6,2},{8,12},{10,14},{12,8},{14,10},{16,20},{18,... | collective-permute-start | bytes 393224 | tf_op jit(solution)/shard_map/ppermute | solution.py:151
  68.2 4.3 %collective-permute-start.3 = (bf16[2,64,256]{2,1,0:T(8,128)(2,1)S(1)}, bf16[2,64,256]{2,1,0:T(8,128)(2,1)S(1)}, u32[]{:S(2)}, u32[]{:S(2)}) collective-permute-start(bf16[2,64,256]{2,1,0:T(8,128)(2,1)S(1)} %fusion.11), channel_id=1, source_target_pairs={{0,8},{2,10},{4,12},{6,14},{8,0},{10,2},{12,4},{14,6},{16,24},{18,... | collective-permute-start | bytes 196616 | tf_op jit(solution)/shard_map/ppermute | solution.py:151
  70.1 5.0 %collective-permute-start.7 = (bf16[2,64,256]{2,1,0:T(8,128)(2,1)S(1)}, bf16[2,64,256]{2,1,0:T(8,128)(2,1)S(1)}, u32[]{:S(2)}, u32[]{:S(2)}) collective-permute-start(bf16[2,64,256]{2,1,0:T(8,128)(2,1)S(1)} %fusion.12), channel_id=1, source_target_pairs={{0,8},{2,10},{4,12},{6,14},{8,0},{10,2},{12,4},{14,6},{16,24},{18,... | collective-permute-start | bytes 196616 | tf_op jit(solution)/shard_map/ppermute | solution.py:151
  72.5 4.9 %collective-permute-start.4 = (bf16[1,64,256]{2,1,0:T(8,128)(2,1)S(1)}, bf16[1,64,256]{2,1,0:T(8,128)(2,1)S(1)}, u32[]{:S(2)}, u32[]{:S(2)}) collective-permute-start(bf16[1,64,256]{2,1,0:T(8,128)(2,1)S(1)} %fusion.15), channel_id=1, source_target_pairs={{0,16},{2,18},{4,20},{6,22},{8,24},{10,26},{12,28},{14,30},{16,0},... | collective-permute-start | bytes 98312 | tf_op jit(solution)/shard_map/ppermute | solution.py:151
  75.1 4.9 %collective-permute-start.8 = (bf16[1,64,256]{2,1,0:T(8,128)(2,1)S(1)}, bf16[1,64,256]{2,1,0:T(8,128)(2,1)S(1)}, u32[]{:S(2)}, u32[]{:S(2)}) collective-permute-start(bf16[1,64,256]{2,1,0:T(8,128)(2,1)S(1)} %fusion.16), channel_id=1, source_target_pairs={{0,16},{2,18},{4,20},{6,22},{8,24},{10,26},{12,28},{14,30},{16,0},... | collective-permute-start | bytes 98312 | tf_op jit(solution)/shard_map/ppermute | solution.py:151

commit v3 on v2

--- a/solution.py
+++ b/solution.py
@@ -83,16 +83,17 @@
             lane < LANES - rest, parts[t], parts[t + 1]
         )
 
-    unroll = 16
+    unroll = 32
 
     @pl.loop(0, width // unroll)
     def _(group):
-        for m in range(unroll):
-            slot = group * unroll + m
-            place = ids_ref[index * width + slot]
-            rows[pl.ds(pl.multiple_of(place * chunks, chunks), chunks), :] = band[
-                pl.ds(pl.multiple_of(slot * chunks, chunks), chunks), :
-            ]
+        slots = [group * unroll + m for m in range(unroll)]
+        places = [ids_ref[index * width + slot] for slot in slots]
+        values = [
+            band[pl.ds(pl.multiple_of(slot * chunks, chunks), chunks), :] for slot in slots
+        ]
+        for place, value in zip(places, values):
+            rows[pl.ds(pl.multiple_of(place * chunks, chunks), chunks), :] = value
 
 
 def whole_kernel(lags_ref, ids_ref, arrived_ref, weights_ref, out_ref, sources, band, rows):

time: 81.2 us -> 81 us (level)
  no operation moved by 1% of the time
where the time goes in v3:
time: 81 us; the launch traced here: 80.5 us
  waiting for transfers between devices  28.6 us (35%)
  starting transfers between devices  20.8 us (26%)
  Pallas kernels  19.8 us (24%)
  other arithmetic  8.07 us (10%)
  local copies, waits for them, and re-layouts  3.04 us (4%)
    pallas_call x1, Pallas kernels, banded_call(): pl.pallas_call(kernel, out_shape=outs, grid_spec=pltpu.PrefetchScalarGrid...  17.1 us
    ppermute x9, waiting for transfers between devices, halve(): return kept + lax.ppermute(sent, axis, partners).astype(jnp.float32)  14.4 us
    all_to_all x1, waiting for transfers between devices, local(): lax.all_to_all(outgoing, 'cfd', split_axis=0, concat_axis=0, tiled=True)  14.3 us
    ppermute x9, starting transfers between devices, halve(): return kept + lax.ppermute(sent, axis, partners).astype(jnp.float32)  13.4 us
    all_to_all x1, starting transfers between devices, local(): lax.all_to_all(outgoing, 'cfd', split_axis=0, concat_axis=0, tiled=True)  7.39 us
    convert_element_type x9, other arithmetic, halve(): sent = jnp.where(mine == 1, first, second).astype(jnp.bfloat16)  3.32 us
    add x5, other arithmetic, halve(): return kept + lax.ppermute(sent, axis, partners).astype(jnp.float32)  3.2 us
    pallas_call x1, Pallas kernels, prepare(): pl.pallas_call(prepare_kernel, out_shape=jax.ShapeDtypeStruct((2 * faces,...  2.72 us
  transfers between devices with their start and end apart: 10, of which 7 were waited for; matrix products, arithmetic and copies ran while one was open for 1% of the time, Pallas kernels for 0%

profile of v3, /device:TPU:0, one launch (start us, length us, event | category | flops | bytes accessed | tf_op | source)
XLA Modules:
  0.0 80.5 jit_solution(14402553989500899036)
XLA Ops:
  0.0 0.7 multiply_bitcast_fusion
  0.7 0.1 broadcast_add_fusion
  0.7 0.1 iota_add_fusion
  0.8 0.8 add.84.src_ref
  1.6 1.4 %copy.32 = f32[3,128]{0,1:T(8,128)} copy(bf16[3,128]{1,0:T(4,128)(2,1)} %param.7) | data formatting | bytes 2304 | tf_op jit(solution)/shard_map/convert_element_type | solution.py:39
  3.0 2.7 %prepare.1 = bf16[256,1024]{1,0:T(8,128)(2,1)} custom-call(s32[256,1]{1,0:T(8,128)} %add.84.src_ref, f32[128,3]{1,0:T(8,128)} %bitcast.149, bf16[5,128,1024]{2,1,0:T(8,128)(2,1)} %surface_ref.1), custom_call_target="tpu_custom_call" | custom-call | tf_op jit(solution)/shard_map/prepare/pallas_call | solution.py:35
  5.7 7.4 %all-to-all-start = ((bf16[16,16,1024]{2,1,0:T(8,128)(2,1)}), bf16[16,16,1024]{2,1,0:T(8,128)(2,1)S(1)}, u32[]{:S(2)}, u32[]{:S(2)}) async-start(bf16[16,16,1024]{2,1,0:T(8,128)(2,1)} %bitcast.144), calls=%async_computation | async-start | bytes 1048576 | tf_op jit(solution)/shard_map/all_to_all | solution.py:173
  13.1 14.3 %all-to-all-done = bf16[16,16,1024]{2,1,0:T(8,128)(2,1)S(1)} async-done(((bf16[16,16,1024]{2,1,0:T(8,128)(2,1)}), bf16[16,16,1024]{2,1,0:T(8,128)(2,1)S(1)}, u32[]{:S(2)}, u32[]{:S(2)}) %all-to-all-start) | async-done | bytes 524320 | tf_op jit(solution)/shard_map/all_to_all | solution.py:173
  27.4 0.0 copy-start
  27.4 0.8 copy-done
  28.2 17.1 %bands.1 = f32[2048,512]{1,0:T(8,128)} custom-call(s32[16]{0:T(128)} %lags_ref.1, s32[2048]{0:T(1024)} %bitcast.150, bf16[16,2,8,1024]{3,2,1,0:T(8,128)(2,1)} %bitcast.143, bf16[2,3,2048,128]{3,2,1,0:T(8,128)(2,1)} %weights_ref.1), custom_call_target="tpu_custom_call" | custom-call | tf_op jit(solution)/shard_map/bands/pallas_call | solution.py:116
  45.3 2.4 %fusion = bf16[8,128,512]{2,1,0:T(8,128)(2,1)S(1)} fusion(f32[8,2,128,512]{3,2,1,0:T(8,128)} %bitcast.137, pred[]{:T(512)S(6)} %eq.14), kind=kLoop, calls=%fused_computation.4 | loop fusion | flops 524288 | bytes 3145729 | tf_op jit(solution)/shard_map/convert_element_type | solution.py:150
  47.7 0.2 collective-permute-start
  47.9 2.5 %collective-permute-done = bf16[8,128,512]{2,1,0:T(8,128)(2,1)S(1)} collective-permute-done((bf16[8,128,512]{2,1,0:T(8,128)(2,1)S(1)}, bf16[8,128,512]{2,1,0:T(8,128)(2,1)S(1)}, u32[]{:S(2)}, u32[]{:S(2)}) %collective-permute-start) | collective-permute-done | bytes 1048608 | tf_op jit(solution)/shard_map/ppermute | solution.py:152
  50.4 2.9 %bitcast_add_fusion = f32[8,128,512]{2,1,0:T(8,128)S(1)} fusion(bf16[8,128,512]{2,1,0:T(8,128)(2,1)S(1)} %collective-permute-done, f32[8,2,128,512]{3,2,1,0:T(8,128)} %bitcast.138, pred[]{:T(512)S(6)} %eq.14), kind=kLoop, calls=%fused_computation.2 | loop fusion | flops 1572864 | bytes 7340033 | tf_op jit(solution)/shard_map/add | solution.py:152
  53.3 0.1 split.21
  53.4 0.8 fusion.3
  54.2 1.0 %collective-permute-start.1 = (bf16[4,64,512]{2,1,0:T(8,128)(2,1)}, bf16[4,64,512]{2,1,0:T(8,128)(2,1)S(1)}, u32[]{:S(2)}, u32[]{:S(2)}) collective-permute-start(bf16[4,64,512]{2,1,0:T(8,128)(2,1)} %fusion.3), channel_id=1, source_target_pairs={{0,4},{2,6},{4,0},{6,2},{8,12},{10,14},{12,8},{14,10},{16,20},{18,... | collective-permute-start | bytes 786440 | tf_op jit(solution)/shard_map/ppermute | solution.py:152
  55.3 1.6 %collective-permute-start.5 = (bf16[8,64,256]{2,1,0:T(8,128)(2,1)S(1)}, bf16[8,64,256]{2,1,0:T(8,128)(2,1)S(1)}, u32[]{:S(2)}, u32[]{:S(2)}) collective-permute-start(bf16[8,64,256]{2,1,0:T(8,128)(2,1)S(1)} %select_convert_fusion.1), channel_id=1, source_target_pairs={{0,1},{1,0},{2,3},{3,2},{4,5},{5,4},{6,7},{7,6},{8,9},{9,8},{10,11... | collective-permute-start | bytes 786440 | tf_op jit(solution)/shard_map/ppermute | solution.py:152
  56.9 5.9 %collective-permute-done.1 = bf16[4,64,512]{2,1,0:T(8,128)(2,1)S(1)} collective-permute-done((bf16[4,64,512]{2,1,0:T(8,128)(2,1)}, bf16[4,64,512]{2,1,0:T(8,128)(2,1)S(1)}, u32[]{:S(2)}, u32[]{:S(2)}) %collective-permute-start.1) | collective-permute-done | bytes 262176 | tf_op jit(solution)/shard_map/ppermute | solution.py:152
  62.7 0.1 fusion.2
  62.9 1.6 %collective-permute-start.2 = (bf16[4,64,256]{2,1,0:T(8,128)(2,1)S(1)}, bf16[4,64,256]{2,1,0:T(8,128)(2,1)S(1)}, u32[]{:S(2)}, u32[]{:S(2)}) collective-permute-start(bf16[4,64,256]{2,1,0:T(8,128)(2,1)S(1)} %select_convert_fusion.4), channel_id=1, source_target_pairs={{0,1},{1,0},{2,3},{3,2},{4,5},{5,4},{6,7},{7,6},{8,9},{9,8},{10,11... | collective-permute-start | bytes 393224 | tf_op jit(solution)/shard_map/ppermute | solution.py:152
  64.5 0.0 collective-permute-done.5
  64.5 0.1 convert_add_fusion
  64.6 1.3 %collective-permute-start.6 = (bf16[4,64,256]{2,1,0:T(8,128)(2,1)S(1)}, bf16[4,64,256]{2,1,0:T(8,128)(2,1)S(1)}, u32[]{:S(2)}, u32[]{:S(2)}) collective-permute-start(bf16[4,64,256]{2,1,0:T(8,128)(2,1)S(1)} %fusion.6), channel_id=1, source_target_pairs={{0,4},{2,6},{4,0},{6,2},{8,12},{10,14},{12,8},{14,10},{16,20},{18,... | collective-permute-start | bytes 393224 | tf_op jit(solution)/shard_map/ppermute | solution.py:152
  66.0 2.0 %collective-permute-done.2 = bf16[4,64,256]{2,1,0:T(8,128)(2,1)S(1)} collective-permute-done((bf16[4,64,256]{2,1,0:T(8,128)(2,1)S(1)}, bf16[4,64,256]{2,1,0:T(8,128)(2,1)S(1)}, u32[]{:S(2)}, u32[]{:S(2)}) %collective-permute-start.2) | collective-permute-done | bytes 131104 | tf_op jit(solution)/shard_map/ppermute | solution.py:152
  68.0 1.8 %collective-permute-start.3 = (bf16[2,64,256]{2,1,0:T(8,128)(2,1)S(1)}, bf16[2,64,256]{2,1,0:T(8,128)(2,1)S(1)}, u32[]{:S(2)}, u32[]{:S(2)}) collective-permute-start(bf16[2,64,256]{2,1,0:T(8,128)(2,1)S(1)} %fusion.11), channel_id=1, source_target_pairs={{0,8},{2,10},{4,12},{6,14},{8,0},{10,2},{12,4},{14,6},{16,24},{18,... | collective-permute-start | bytes 196616 | tf_op jit(solution)/shard_map/ppermute | solution.py:152
  69.8 0.0 collective-permute-done.6
  69.9 1.6 %collective-permute-start.7 = (bf16[2,64,256]{2,1,0:T(8,128)(2,1)S(1)}, bf16[2,64,256]{2,1,0:T(8,128)(2,1)S(1)}, u32[]{:S(2)}, u32[]{:S(2)}) collective-permute-start(bf16[2,64,256]{2,1,0:T(8,128)(2,1)S(1)} %fusion.12), channel_id=1, source_target_pairs={{0,8},{2,10},{4,12},{6,14},{8,0},{10,2},{12,4},{14,6},{16,24},{18,... | collective-permute-start | bytes 196616 | tf_op jit(solution)/shard_map/ppermute | solution.py:152
  71.6 0.8 collective-permute-done.3
  72.4 2.5 %collective-permute-start.4 = (bf16[1,64,256]{2,1,0:T(8,128)(2,1)S(1)}, bf16[1,64,256]{2,1,0:T(8,128)(2,1)S(1)}, u32[]{:S(2)}, u32[]{:S(2)}) collective-permute-start(bf16[1,64,256]{2,1,0:T(8,128)(2,1)S(1)} %fusion.15), channel_id=1, source_target_pairs={{0,16},{2,18},{4,20},{6,22},{8,24},{10,26},{12,28},{14,30},{16,0},... | collective-permute-start | bytes 98312 | tf_op jit(solution)/shard_map/ppermute | solution.py:152
  74.9 0.0 collective-permute-done.7
  74.9 1.7 %collective-permute-start.8 = (bf16[1,64,256]{2,1,0:T(8,128)(2,1)S(1)}, bf16[1,64,256]{2,1,0:T(8,128)(2,1)S(1)}, u32[]{:S(2)}, u32[]{:S(2)}) collective-permute-start(bf16[1,64,256]{2,1,0:T(8,128)(2,1)S(1)} %fusion.16), channel_id=1, source_target_pairs={{0,16},{2,18},{4,20},{6,22},{8,24},{10,26},{12,28},{14,30},{16,0},... | collective-permute-start | bytes 98312 | tf_op jit(solution)/shard_map/ppermute | solution.py:152
  76.6 0.7 collective-permute-done.4
  77.3 2.5 %collective-permute-done.8 = bf16[1,64,256]{2,1,0:T(8,128)(2,1)S(1)} collective-permute-done((bf16[1,64,256]{2,1,0:T(8,128)(2,1)S(1)}, bf16[1,64,256]{2,1,0:T(8,128)(2,1)S(1)}, u32[]{:S(2)}, u32[]{:S(2)}) %collective-permute-start.8) | collective-permute-done | bytes 32800 | tf_op jit(solution)/shard_map/ppermute | solution.py:152
  79.8 0.7 pad_maximum_fusion
  (14 shorter events, 0.3 us)
Async XLA Ops:
  5.7 21.7 %all-to-all-start = ((bf16[16,16,1024]{2,1,0:T(8,128)(2,1)}), bf16[16,16,1024]{2,1,0:T(8,128)(2,1)S(1)}, u32[]{:S(2)}, u32[]{:S(2)}) async-start(bf16[16,16,1024]{2,1,0:T(8,128)(2,1)} %bitcast.144), calls=%async_computation | async-start | bytes 1048576 | tf_op jit(solution)/shard_map/all_to_all | solution.py:173
  27.4 0.8 copy-start
  47.7 2.7 %collective-permute-start = (bf16[8,128,512]{2,1,0:T(8,128)(2,1)S(1)}, bf16[8,128,512]{2,1,0:T(8,128)(2,1)S(1)}, u32[]{:S(2)}, u32[]{:S(2)}) collective-permute-start(bf16[8,128,512]{2,1,0:T(8,128)(2,1)S(1)} %fusion), channel_id=1, source_target_pairs={{0,2},{2,0},{4,6},{6,4},{8,10},{10,8},{12,14},{14,12},{16,18},{18,... | collective-permute-start | bytes 3145736 | tf_op jit(solution)/shard_map/ppermute | solution.py:152
  54.2 8.6 %collective-permute-start.1 = (bf16[4,64,512]{2,1,0:T(8,128)(2,1)}, bf16[4,64,512]{2,1,0:T(8,128)(2,1)S(1)}, u32[]{:S(2)}, u32[]{:S(2)}) collective-permute-start(bf16[4,64,512]{2,1,0:T(8,128)(2,1)} %fusion.3), channel_id=1, source_target_pairs={{0,4},{2,6},{4,0},{6,2},{8,12},{10,14},{12,8},{14,10},{16,20},{18,... | collective-permute-start | bytes 786440 | tf_op jit(solution)/shard_map/ppermute | solution.py:152
  55.3 9.2 %collective-permute-start.5 = (bf16[8,64,256]{2,1,0:T(8,128)(2,1)S(1)}, bf16[8,64,256]{2,1,0:T(8,128)(2,1)S(1)}, u32[]{:S(2)}, u32[]{:S(2)}) collective-permute-start(bf16[8,64,256]{2,1,0:T(8,128)(2,1)S(1)} %select_convert_fusion.1), channel_id=1, source_target_pairs={{0,1},{1,0},{2,3},{3,2},{4,5},{5,4},{6,7},{7,6},{8,9},{9,8},{10,11... | collective-permute-start | bytes 786440 | tf_op jit(solution)/shard_map/ppermute | solution.py:152
  62.9 5.0 %collective-permute-start.2 = (bf16[4,64,256]{2,1,0:T(8,128)(2,1)S(1)}, bf16[4,64,256]{2,1,0:T(8,128)(2,1)S(1)}, u32[]{:S(2)}, u32[]{:S(2)}) collective-permute-start(bf16[4,64,256]{2,1,0:T(8,128)(2,1)S(1)} %select_convert_fusion.4), channel_id=1, source_target_pairs={{0,1},{1,0},{2,3},{3,2},{4,5},{5,4},{6,7},{7,6},{8,9},{9,8},{10,11... | collective-permute-start | bytes 393224 | tf_op jit(solution)/shard_map/ppermute | solution.py:152
  64.6 5.2 %collective-permute-start.6 = (bf16[4,64,256]{2,1,0:T(8,128)(2,1)S(1)}, bf16[4,64,256]{2,1,0:T(8,128)(2,1)S(1)}, u32[]{:S(2)}, u32[]{:S(2)}) collective-permute-start(bf16[4,64,256]{2,1,0:T(8,128)(2,1)S(1)} %fusion.6), channel_id=1, source_target_pairs={{0,4},{2,6},{4,0},{6,2},{8,12},{10,14},{12,8},{14,10},{16,20},{18,... | collective-permute-start | bytes 393224 | tf_op jit(solution)/shard_map/ppermute | solution.py:152
  68.0 4.3 %collective-permute-start.3 = (bf16[2,64,256]{2,1,0:T(8,128)(2,1)S(1)}, bf16[2,64,256]{2,1,0:T(8,128)(2,1)S(1)}, u32[]{:S(2)}, u32[]{:S(2)}) collective-permute-start(bf16[2,64,256]{2,1,0:T(8,128)(2,1)S(1)} %fusion.11), channel_id=1, source_target_pairs={{0,8},{2,10},{4,12},{6,14},{8,0},{10,2},{12,4},{14,6},{16,24},{18,... | collective-permute-start | bytes 196616 | tf_op jit(solution)/shard_map/ppermute | solution.py:152
  69.9 5.0 %collective-permute-start.7 = (bf16[2,64,256]{2,1,0:T(8,128)(2,1)S(1)}, bf16[2,64,256]{2,1,0:T(8,128)(2,1)S(1)}, u32[]{:S(2)}, u32[]{:S(2)}) collective-permute-start(bf16[2,64,256]{2,1,0:T(8,128)(2,1)S(1)} %fusion.12), channel_id=1, source_target_pairs={{0,8},{2,10},{4,12},{6,14},{8,0},{10,2},{12,4},{14,6},{16,24},{18,... | collective-permute-start | bytes 196616 | tf_op jit(solution)/shard_map/ppermute | solution.py:152
  72.4 4.9 %collective-permute-start.4 = (bf16[1,64,256]{2,1,0:T(8,128)(2,1)S(1)}, bf16[1,64,256]{2,1,0:T(8,128)(2,1)S(1)}, u32[]{:S(2)}, u32[]{:S(2)}) collective-permute-start(bf16[1,64,256]{2,1,0:T(8,128)(2,1)S(1)} %fusion.15), channel_id=1, source_target_pairs={{0,16},{2,18},{4,20},{6,22},{8,24},{10,26},{12,28},{14,30},{16,0},... | collective-permute-start | bytes 98312 | tf_op jit(solution)/shard_map/ppermute | solution.py:152
  74.9 4.9 %collective-permute-start.8 = (bf16[1,64,256]{2,1,0:T(8,128)(2,1)S(1)}, bf16[1,64,256]{2,1,0:T(8,128)(2,1)S(1)}, u32[]{:S(2)}, u32[]{:S(2)}) collective-permute-start(bf16[1,64,256]{2,1,0:T(8,128)(2,1)S(1)} %fusion.16), channel_id=1, source_target_pairs={{0,16},{2,18},{4,20},{6,22},{8,24},{10,26},{12,28},{14,30},{16,0},... | collective-permute-start | bytes 98312 | tf_op jit(solution)/shard_map/ppermute | solution.py:152

commit v4 on v3

--- a/solution.py
+++ b/solution.py
@@ -96,18 +96,26 @@
             rows[pl.ds(pl.multiple_of(place * chunks, chunks), chunks), :] = value
 
 
-def whole_kernel(lags_ref, ids_ref, arrived_ref, weights_ref, out_ref, sources, band, rows):
+def halves_kernel(
+    lags_ref, ids_ref, mine_ref, arrived_ref, weights_ref, kept_ref, sent_ref, sources, band, rows
+):
     scatter_bands(lags_ref, ids_ref, arrived_ref, weights_ref, sources, band, rows)
-    observers, out_len = out_ref.shape
+    pairs, height, out_len = kept_ref.shape
     chunks = out_len // LANES
+    mine = mine_ref[0]
 
     @pl.when(pl.program_id(0) == pl.num_programs(0) - 1)
     def _():
-        for t in range(chunks):
-            out_ref[:, t * LANES : (t + 1) * LANES] = rows[pl.ds(t, observers, stride=chunks), :]
-
-
-def banded_call(kernel, outs, arrived, kernel_weights, band_observers, band_lags):
+        for pair in range(pairs):
+            for t in range(chunks):
+                lanes = slice(t * LANES, (t + 1) * LANES)
+                for out, owner in ((kept_ref, 2 * pair + mine), (sent_ref, 2 * pair + 1 - mine)):
+                    first = pl.multiple_of(owner * (height * chunks), height * chunks)
+                    part = rows[pl.ds(first + t, height, stride=chunks), :]
+                    out[pair, :, lanes] = part.astype(out.dtype)
+
+
+def banded_call(kernel, outs, arrived, kernel_weights, band_observers, band_lags, mine):
     taps, terms, observers, faces = kernel_weights.shape
     bands, width = band_observers.shape
     steps = arrived.shape[-1]
@@ -117,7 +125,7 @@
         kernel,
         out_shape=outs,
         grid_spec=pltpu.PrefetchScalarGridSpec(
-            num_scalar_prefetch=2,
+            num_scalar_prefetch=3,
             grid=(bands,),
             in_specs=[
                 pl.BlockSpec(arrived.shape, lambda b, *_: (0,) * rank),
@@ -134,7 +142,7 @@
         ),
         compiler_params=pltpu.CompilerParams(dimension_semantics=("arbitrary",)),
         name="bands",
-    )(band_lags, band_observers.reshape(-1), arrived, kernel_weights)
+    )(band_lags, band_observers.reshape(-1), mine, arrived, kernel_weights)
 
 
 def halve(total, axis, bit):
@@ -152,13 +160,13 @@
     return kept + lax.ppermute(sent, axis, partners).astype(jnp.float32)
 
 
-def exchange_sums(partial_value):
+def exchange_sums(kept, sent):
     owners = lax.axis_size("cfd")
-    observers, times = partial_value.shape
     near = [("cfd", b) for b in range(owners.bit_length() - 1)]
     across = [("ac", b) for b in reversed(range(lax.axis_size("ac").bit_length() - 1))]
     orders = (near[:2] + across + near[2:], near[:1] + across + near[1:])
-    total = halve(partial_value.reshape(owners, observers // owners, times), *near[0])
+    partners = [(i, i ^ 1) for i in range(owners)]
+    total = kept + lax.ppermute(sent, "cfd", partners).astype(jnp.float32)
     streams = jnp.split(total, len(orders), axis=1)
     for step in range(1, len(near) + len(across)):
         streams = [halve(part, *order[step]) for part, order in zip(streams, orders)]
@@ -174,15 +182,17 @@
     arrived = arrived.reshape(blocks, 2, size, steps)
     if size % 8:
         arrived = arrived.transpose(1, 0, 2, 3).reshape(2 * faces, steps)
-    partial_value = banded_call(
-        whole_kernel,
-        jax.ShapeDtypeStruct((kernel_weights.shape[2], steps // 2), jnp.float32),
+    shape = (blocks // 2, kernel_weights.shape[2] // blocks, steps // 2)
+    kept, sent = banded_call(
+        halves_kernel,
+        [jax.ShapeDtypeStruct(shape, kind) for kind in (jnp.float32, jnp.bfloat16)],
         arrived,
         kernel_weights,
         band_observers,
         band_lags,
-    )
-    return exchange_sums(partial_value)
+        (lax.axis_index("cfd") & 1).astype(jnp.int32).reshape(1),
+    )
+    return exchange_sums(kept, sent)
 
 
 def solution(mesh):

time: 81 us -> 77.5 us (0.957)
  other arithmetic: 8.07 us -> 4.73 us
    add x5 -> x4, other arithmetic: 3.2 us -> 0.3 us  [halve(): return kept + lax.ppermute(sent, axis, partners).astype(jnp.float32)]
    ppermute x0 -> x1, waiting for transfers between devices: none -> 2.75 us  [exchange_sums(): total = kept + lax.ppermute(sent, 'cfd', partners).astype(jnp.float32)]
    ppermute x9 -> x8, waiting for transfers between devices: 14.4 us -> 11.9 us  [halve(): return kept + lax.ppermute(sent, axis, partners).astype(jnp.float32)]
    convert_element_type x9 -> x8, other arithmetic: 3.32 us -> 0.91 us  [halve(): sent = jnp.where(mine == 1, first, second).astype(jnp.bfloat16)]
    add x0 -> x1, other arithmetic: none -> 1.98 us  [exchange_sums(): total = kept + lax.ppermute(sent, 'cfd', partners).astype(jnp.float32)]
    ppermute x9 -> x8, starting transfers between devices: 13.4 us -> 13.1 us  [halve(): return kept + lax.ppermute(sent, axis, partners).astype(jnp.float32)]
where the time goes in v4:
time: 77.5 us; the launch traced here: 76.9 us
  waiting for transfers between devices  28.9 us (37%)
  starting transfers between devices  20.6 us (27%)
  Pallas kernels  19.5 us (25%)
  other arithmetic  4.73 us (6%)
  local copies, waits for them, and re-layouts  3.06 us (4%)
    pallas_call x1, Pallas kernels, banded_call(): pl.pallas_call(kernel, out_shape=outs, grid_spec=pltpu.PrefetchScalarGrid...  16.7 us
    all_to_all x1, waiting for transfers between devices, local(): lax.all_to_all(outgoing, 'cfd', split_axis=0, concat_axis=0, tiled=True)  14.3 us
    ppermute x8, starting transfers between devices, halve(): return kept + lax.ppermute(sent, axis, partners).astype(jnp.float32)  13.1 us
    ppermute x8, waiting for transfers between devices, halve(): return kept + lax.ppermute(sent, axis, partners).astype(jnp.float32)  11.9 us
    all_to_all x1, starting transfers between devices, local(): lax.all_to_all(outgoing, 'cfd', split_axis=0, concat_axis=0, tiled=True)  7.39 us
    ppermute x1, waiting for transfers between devices, exchange_sums(): total = kept + lax.ppermute(sent, 'cfd', partners).astype(jnp.float32)  2.75 us
    pallas_call x1, Pallas kernels, prepare(): pl.pallas_call(prepare_kernel, out_shape=jax.ShapeDtypeStruct((2 * faces,...  2.74 us
    add x1, other arithmetic, exchange_sums(): total = kept + lax.ppermute(sent, 'cfd', partners).astype(jnp.float32)  1.98 us
  transfers between devices with their start and end apart: 10, of which 7 were waited for; matrix products, arithmetic and copies ran while one was open for 1% of the time, Pallas kernels for 0%

profile of v4, /device:TPU:0, one launch (start us, length us, event | category | flops | bytes accessed | tf_op | source)
XLA Modules:
  0.0 76.9 jit_solution(6417355379833056607)
XLA Ops:
  0.0 0.7 multiply_bitcast_fusion
  0.7 0.1 broadcast_add_fusion
  0.7 0.1 iota_add_fusion
  0.8 0.8 add.84.src_ref
  1.6 1.4 %copy.16 = f32[3,128]{0,1:T(8,128)} copy(bf16[3,128]{1,0:T(4,128)(2,1)} %param.7) | data formatting | bytes 2304 | tf_op jit(solution)/shard_map/convert_element_type | solution.py:39
  3.0 2.7 %prepare.1 = bf16[256,1024]{1,0:T(8,128)(2,1)} custom-call(s32[256,1]{1,0:T(8,128)} %add.84.src_ref, f32[128,3]{1,0:T(8,128)} %bitcast.127, bf16[5,128,1024]{2,1,0:T(8,128)(2,1)} %surface_ref.1), custom_call_target="tpu_custom_call" | custom-call | tf_op jit(solution)/shard_map/prepare/pallas_call | solution.py:35
  5.7 7.4 %all-to-all-start = ((bf16[16,16,1024]{2,1,0:T(8,128)(2,1)}), bf16[16,16,1024]{2,1,0:T(8,128)(2,1)S(1)}, u32[]{:S(2)}, u32[]{:S(2)}) async-start(bf16[16,16,1024]{2,1,0:T(8,128)(2,1)} %bitcast.122), calls=%async_computation | async-start | bytes 1048576 | tf_op jit(solution)/shard_map/all_to_all | solution.py:181
  13.1 14.3 %all-to-all-done = bf16[16,16,1024]{2,1,0:T(8,128)(2,1)S(1)} async-done(((bf16[16,16,1024]{2,1,0:T(8,128)(2,1)}), bf16[16,16,1024]{2,1,0:T(8,128)(2,1)S(1)}, u32[]{:S(2)}, u32[]{:S(2)}) %all-to-all-start) | async-done | bytes 524320 | tf_op jit(solution)/shard_map/all_to_all | solution.py:181
  27.4 0.0 copy-start
  27.4 0.8 %copy-done = bf16[16,16,1024]{2,1,0:T(8,128)(2,1)} copy-done((bf16[16,16,1024]{2,1,0:T(8,128)(2,1)}, bf16[16,16,1024]{2,1,0:T(8,128)(2,1)S(1)}, u32[]{:S(2)}) %copy-start) | copy-done | bytes 524312
  28.2 16.7 %bands.1 = (f32[8,128,512]{2,1,0:T(8,128)}, bf16[8,128,512]{2,1,0:T(8,128)(2,1)}) custom-call(s32[16]{0:T(128)} %lags_ref.1, s32[2048]{0:T(1024)} %bitcast.128, s32[1]{0:T(128)} %bitcast.1.mine_ref, bf16[16,2,8,1024]{3,2,1,0:T(8,128)(2,1)} %bitcast.121, bf16[2,3,2048,128]{3,2,1,0:T(8,128)(2,1)} %weights_ref.1), custom_call_target="tpu_custom_call" | custom-call | tf_op jit(solution)/shard_map/bands/pallas_call | solution.py:124
  45.0 0.1 collective-permute-start
  45.1 2.8 %collective-permute-done = bf16[8,128,512]{2,1,0:T(8,128)(2,1)S(1)} collective-permute-done((bf16[8,128,512]{2,1,0:T(8,128)(2,1)}, bf16[8,128,512]{2,1,0:T(8,128)(2,1)S(1)}, u32[]{:S(2)}, u32[]{:S(2)}) %collective-permute-start) | collective-permute-done | bytes 1048608 | tf_op jit(solution)/shard_map/ppermute | solution.py:169
  47.8 2.0 %convert_add_fusion = f32[8,128,512]{2,1,0:T(8,128)S(1)} fusion(f32[8,128,512]{2,1,0:T(8,128)} %get-tuple-element.7, bf16[8,128,512]{2,1,0:T(8,128)(2,1)S(1)} %collective-permute-done), kind=kLoop, calls=%fused_computation | loop fusion | flops 1048576 | bytes 5242880 | tf_op jit(solution)/shard_map/add | solution.py:169
  49.8 0.1 split.21
  49.9 0.8 fusion
  50.7 1.0 %collective-permute-start.1 = (bf16[4,64,512]{2,1,0:T(8,128)(2,1)}, bf16[4,64,512]{2,1,0:T(8,128)(2,1)S(1)}, u32[]{:S(2)}, u32[]{:S(2)}) collective-permute-start(bf16[4,64,512]{2,1,0:T(8,128)(2,1)} %fusion), channel_id=1, source_target_pairs={{0,4},{2,6},{4,0},{6,2},{8,12},{10,14},{12,8},{14,10},{16,20},{18,... | collective-permute-start | bytes 786440 | tf_op jit(solution)/shard_map/ppermute | solution.py:160
  51.7 1.6 %collective-permute-start.5 = (bf16[8,64,256]{2,1,0:T(8,128)(2,1)S(1)}, bf16[8,64,256]{2,1,0:T(8,128)(2,1)S(1)}, u32[]{:S(2)}, u32[]{:S(2)}) collective-permute-start(bf16[8,64,256]{2,1,0:T(8,128)(2,1)S(1)} %select_convert_fusion), channel_id=1, source_target_pairs={{0,1},{1,0},{2,3},{3,2},{4,5},{5,4},{6,7},{7,6},{8,9},{9,8},{10,11... | collective-permute-start | bytes 786440 | tf_op jit(solution)/shard_map/ppermute | solution.py:160
  53.3 5.9 %collective-permute-done.1 = bf16[4,64,512]{2,1,0:T(8,128)(2,1)S(1)} collective-permute-done((bf16[4,64,512]{2,1,0:T(8,128)(2,1)}, bf16[4,64,512]{2,1,0:T(8,128)(2,1)S(1)}, u32[]{:S(2)}, u32[]{:S(2)}) %collective-permute-start.1) | collective-permute-done | bytes 262176 | tf_op jit(solution)/shard_map/ppermute | solution.py:160
  59.2 0.1 bitcast_add_fusion
  59.4 1.6 %collective-permute-start.2 = (bf16[4,64,256]{2,1,0:T(8,128)(2,1)S(1)}, bf16[4,64,256]{2,1,0:T(8,128)(2,1)S(1)}, u32[]{:S(2)}, u32[]{:S(2)}) collective-permute-start(bf16[4,64,256]{2,1,0:T(8,128)(2,1)S(1)} %select_convert_fusion.3), channel_id=1, source_target_pairs={{0,1},{1,0},{2,3},{3,2},{4,5},{5,4},{6,7},{7,6},{8,9},{9,8},{10,11... | collective-permute-start | bytes 393224 | tf_op jit(solution)/shard_map/ppermute | solution.py:160
  61.0 0.0 collective-permute-done.5
  61.0 0.1 convert_add_fusion.1
  61.1 1.3 %collective-permute-start.6 = (bf16[4,64,256]{2,1,0:T(8,128)(2,1)S(1)}, bf16[4,64,256]{2,1,0:T(8,128)(2,1)S(1)}, u32[]{:S(2)}, u32[]{:S(2)}) collective-permute-start(bf16[4,64,256]{2,1,0:T(8,128)(2,1)S(1)} %fusion.1), channel_id=1, source_target_pairs={{0,4},{2,6},{4,0},{6,2},{8,12},{10,14},{12,8},{14,10},{16,20},{18,... | collective-permute-start | bytes 393224 | tf_op jit(solution)/shard_map/ppermute | solution.py:160
  62.4 2.0 %collective-permute-done.2 = bf16[4,64,256]{2,1,0:T(8,128)(2,1)S(1)} collective-permute-done((bf16[4,64,256]{2,1,0:T(8,128)(2,1)S(1)}, bf16[4,64,256]{2,1,0:T(8,128)(2,1)S(1)}, u32[]{:S(2)}, u32[]{:S(2)}) %collective-permute-start.2) | collective-permute-done | bytes 131104 | tf_op jit(solution)/shard_map/ppermute | solution.py:160
  64.5 1.8 %collective-permute-start.3 = (bf16[2,64,256]{2,1,0:T(8,128)(2,1)S(1)}, bf16[2,64,256]{2,1,0:T(8,128)(2,1)S(1)}, u32[]{:S(2)}, u32[]{:S(2)}) collective-permute-start(bf16[2,64,256]{2,1,0:T(8,128)(2,1)S(1)} %fusion.6), channel_id=1, source_target_pairs={{0,8},{2,10},{4,12},{6,14},{8,0},{10,2},{12,4},{14,6},{16,24},{18,... | collective-permute-start | bytes 196616 | tf_op jit(solution)/shard_map/ppermute | solution.py:160
  66.3 0.0 collective-permute-done.6
  66.4 1.7 %collective-permute-start.7 = (bf16[2,64,256]{2,1,0:T(8,128)(2,1)S(1)}, bf16[2,64,256]{2,1,0:T(8,128)(2,1)S(1)}, u32[]{:S(2)}, u32[]{:S(2)}) collective-permute-start(bf16[2,64,256]{2,1,0:T(8,128)(2,1)S(1)} %fusion.7), channel_id=1, source_target_pairs={{0,8},{2,10},{4,12},{6,14},{8,0},{10,2},{12,4},{14,6},{16,24},{18,... | collective-permute-start | bytes 196616 | tf_op jit(solution)/shard_map/ppermute | solution.py:160
  68.0 0.8 %collective-permute-done.3 = bf16[2,64,256]{2,1,0:T(8,128)(2,1)S(1)} collective-permute-done((bf16[2,64,256]{2,1,0:T(8,128)(2,1)S(1)}, bf16[2,64,256]{2,1,0:T(8,128)(2,1)S(1)}, u32[]{:S(2)}, u32[]{:S(2)}) %collective-permute-start.3) | collective-permute-done | bytes 65568 | tf_op jit(solution)/shard_map/ppermute | solution.py:160
  68.9 2.5 %collective-permute-start.4 = (bf16[1,64,256]{2,1,0:T(8,128)(2,1)S(1)}, bf16[1,64,256]{2,1,0:T(8,128)(2,1)S(1)}, u32[]{:S(2)}, u32[]{:S(2)}) collective-permute-start(bf16[1,64,256]{2,1,0:T(8,128)(2,1)S(1)} %fusion.10), channel_id=1, source_target_pairs={{0,16},{2,18},{4,20},{6,22},{8,24},{10,26},{12,28},{14,30},{16,0},... | collective-permute-start | bytes 98312 | tf_op jit(solution)/shard_map/ppermute | solution.py:160
  71.3 0.0 collective-permute-done.7
  71.4 1.7 %collective-permute-start.8 = (bf16[1,64,256]{2,1,0:T(8,128)(2,1)S(1)}, bf16[1,64,256]{2,1,0:T(8,128)(2,1)S(1)}, u32[]{:S(2)}, u32[]{:S(2)}) collective-permute-start(bf16[1,64,256]{2,1,0:T(8,128)(2,1)S(1)} %fusion.11), channel_id=1, source_target_pairs={{0,16},{2,18},{4,20},{6,22},{8,24},{10,26},{12,28},{14,30},{16,0},... | collective-permute-start | bytes 98312 | tf_op jit(solution)/shard_map/ppermute | solution.py:160
  73.1 0.7 collective-permute-done.4
  73.8 2.5 %collective-permute-done.8 = bf16[1,64,256]{2,1,0:T(8,128)(2,1)S(1)} collective-permute-done((bf16[1,64,256]{2,1,0:T(8,128)(2,1)S(1)}, bf16[1,64,256]{2,1,0:T(8,128)(2,1)S(1)}, u32[]{:S(2)}, u32[]{:S(2)}) %collective-permute-start.8) | collective-permute-done | bytes 32800 | tf_op jit(solution)/shard_map/ppermute | solution.py:160
  76.3 0.7 pad_maximum_fusion
  (14 shorter events, 0.3 us)
Async XLA Ops:
  5.7 21.7 %all-to-all-start = ((bf16[16,16,1024]{2,1,0:T(8,128)(2,1)}), bf16[16,16,1024]{2,1,0:T(8,128)(2,1)S(1)}, u32[]{:S(2)}, u32[]{:S(2)}) async-start(bf16[16,16,1024]{2,1,0:T(8,128)(2,1)} %bitcast.122), calls=%async_computation | async-start | bytes 1048576 | tf_op jit(solution)/shard_map/all_to_all | solution.py:181
  27.4 0.8 %copy-start = (bf16[16,16,1024]{2,1,0:T(8,128)(2,1)}, bf16[16,16,1024]{2,1,0:T(8,128)(2,1)S(1)}, u32[]{:S(2)}) copy-start(bf16[16,16,1024]{2,1,0:T(8,128)(2,1)S(1)} %all-to-all-done) | copy-start | bytes 1572868
  45.0 2.9 %collective-permute-start = (bf16[8,128,512]{2,1,0:T(8,128)(2,1)}, bf16[8,128,512]{2,1,0:T(8,128)(2,1)S(1)}, u32[]{:S(2)}, u32[]{:S(2)}) collective-permute-start(bf16[8,128,512]{2,1,0:T(8,128)(2,1)} %get-tuple-element.8), channel_id=1, source_target_pairs={{0,2},{2,0},{4,6},{6,4},{8,10},{10,8},{12,14},{14,12},{16,18},{18,... | collective-permute-start | bytes 3145736 | tf_op jit(solution)/shard_map/ppermute | solution.py:169
  50.7 8.6 %collective-permute-start.1 = (bf16[4,64,512]{2,1,0:T(8,128)(2,1)}, bf16[4,64,512]{2,1,0:T(8,128)(2,1)S(1)}, u32[]{:S(2)}, u32[]{:S(2)}) collective-permute-start(bf16[4,64,512]{2,1,0:T(8,128)(2,1)} %fusion), channel_id=1, source_target_pairs={{0,4},{2,6},{4,0},{6,2},{8,12},{10,14},{12,8},{14,10},{16,20},{18,... | collective-permute-start | bytes 786440 | tf_op jit(solution)/shard_map/ppermute | solution.py:160
  51.7 9.2 %collective-permute-start.5 = (bf16[8,64,256]{2,1,0:T(8,128)(2,1)S(1)}, bf16[8,64,256]{2,1,0:T(8,128)(2,1)S(1)}, u32[]{:S(2)}, u32[]{:S(2)}) collective-permute-start(bf16[8,64,256]{2,1,0:T(8,128)(2,1)S(1)} %select_convert_fusion), channel_id=1, source_target_pairs={{0,1},{1,0},{2,3},{3,2},{4,5},{5,4},{6,7},{7,6},{8,9},{9,8},{10,11... | collective-permute-start | bytes 786440 | tf_op jit(solution)/shard_map/ppermute | solution.py:160
  59.4 5.0 %collective-permute-start.2 = (bf16[4,64,256]{2,1,0:T(8,128)(2,1)S(1)}, bf16[4,64,256]{2,1,0:T(8,128)(2,1)S(1)}, u32[]{:S(2)}, u32[]{:S(2)}) collective-permute-start(bf16[4,64,256]{2,1,0:T(8,128)(2,1)S(1)} %select_convert_fusion.3), channel_id=1, source_target_pairs={{0,1},{1,0},{2,3},{3,2},{4,5},{5,4},{6,7},{7,6},{8,9},{9,8},{10,11... | collective-permute-start | bytes 393224 | tf_op jit(solution)/shard_map/ppermute | solution.py:160
  61.1 5.2 %collective-permute-start.6 = (bf16[4,64,256]{2,1,0:T(8,128)(2,1)S(1)}, bf16[4,64,256]{2,1,0:T(8,128)(2,1)S(1)}, u32[]{:S(2)}, u32[]{:S(2)}) collective-permute-start(bf16[4,64,256]{2,1,0:T(8,128)(2,1)S(1)} %fusion.1), channel_id=1, source_target_pairs={{0,4},{2,6},{4,0},{6,2},{8,12},{10,14},{12,8},{14,10},{16,20},{18,... | collective-permute-start | bytes 393224 | tf_op jit(solution)/shard_map/ppermute | solution.py:160
  64.5 4.3 %collective-permute-start.3 = (bf16[2,64,256]{2,1,0:T(8,128)(2,1)S(1)}, bf16[2,64,256]{2,1,0:T(8,128)(2,1)S(1)}, u32[]{:S(2)}, u32[]{:S(2)}) collective-permute-start(bf16[2,64,256]{2,1,0:T(8,128)(2,1)S(1)} %fusion.6), channel_id=1, source_target_pairs={{0,8},{2,10},{4,12},{6,14},{8,0},{10,2},{12,4},{14,6},{16,24},{18,... | collective-permute-start | bytes 196616 | tf_op jit(solution)/shard_map/ppermute | solution.py:160
  66.4 5.0 %collective-permute-start.7 = (bf16[2,64,256]{2,1,0:T(8,128)(2,1)S(1)}, bf16[2,64,256]{2,1,0:T(8,128)(2,1)S(1)}, u32[]{:S(2)}, u32[]{:S(2)}) collective-permute-start(bf16[2,64,256]{2,1,0:T(8,128)(2,1)S(1)} %fusion.7), channel_id=1, source_target_pairs={{0,8},{2,10},{4,12},{6,14},{8,0},{10,2},{12,4},{14,6},{16,24},{18,... | collective-permute-start | bytes 196616 | tf_op jit(solution)/shard_map/ppermute | solution.py:160
  68.9 4.9 %collective-permute-start.4 = (bf16[1,64,256]{2,1,0:T(8,128)(2,1)S(1)}, bf16[1,64,256]{2,1,0:T(8,128)(2,1)S(1)}, u32[]{:S(2)}, u32[]{:S(2)}) collective-permute-start(bf16[1,64,256]{2,1,0:T(8,128)(2,1)S(1)} %fusion.10), channel_id=1, source_target_pairs={{0,16},{2,18},{4,20},{6,22},{8,24},{10,26},{12,28},{14,30},{16,0},... | collective-permute-start | bytes 98312 | tf_op jit(solution)/shard_map/ppermute | solution.py:160
  71.4 4.9 %collective-permute-start.8 = (bf16[1,64,256]{2,1,0:T(8,128)(2,1)S(1)}, bf16[1,64,256]{2,1,0:T(8,128)(2,1)S(1)}, u32[]{:S(2)}, u32[]{:S(2)}) collective-permute-start(bf16[1,64,256]{2,1,0:T(8,128)(2,1)S(1)} %fusion.11), channel_id=1, source_target_pairs={{0,16},{2,18},{4,20},{6,22},{8,24},{10,26},{12,28},{14,30},{16,0},... | collective-permute-start | bytes 98312 | tf_op jit(solution)/shard_map/ppermute | solution.py:160
